TPU v7x, 128 devices: a whole 4x4x4 slice. The times are simulated.
128 devices in a mesh: mem: 16 (over y, x), pix: 8 (over z, core).
Axes of the slice: x: 4, y: 4, z: 4, core: 2. Of those that a mesh axis runs over, the one named last changes fastest.
Arguments:
- prior_motion: bfloat16 [64, 16, 262144], P('mem', None, 'pix'), may hold values from -6 to 6
- measured_motion: float32 [1200], replicated, may hold values from -1.6 to 1.6
- measurement_noise_stddev: float32 [1200], replicated, may hold values from 0.05 to 0.5
- gaussian_jitter: float32 [2, 1200, 64], replicated, may hold values from -6 to 6
- scene_couples: int32 [2, 1200], replicated, may hold values from 0 to 15, as said below
- targeted_tile_number: int32 [1200], replicated, may hold values from 0 to 4095
Outputs:
- analysis: bfloat16 [64, 16, 262144], P('mem', None, 'pix')
Inputs may be any that keep to these rules, and one draw needn't show every extreme that they name: scene_couples[0, k] < scene_couples[1, k]: row 0 holds the earlier acquisition, row 1 the later.
All inputs are finite; a program needn't handle non-finite values.
Results may differ from a plain program's by a relative error of at most 0.011.
Values may be sent and summed in bfloat16 or wider, within the bound.
No kernel may reach another device: no remote copies, remote signals or barrier semaphores. Data moves between devices by JAX's collectives and lax.ppermute only.
A program may use at most 128 MiB of HBM per device.

v0:
```python
import math
import jax
import jax.numpy as jnp
from jax import lax
from jax.sharding import PartitionSpec as P

BLK = 64
PASS_COUNT = 2
HI = lax.Precision.HIGHEST


def mm(a, b):
    return jnp.dot(a, b, precision=HI, preferred_element_type=jnp.float32)


def tn(a, b):
    return lax.dot_general(
        a, b, (((0,), (0,)), ((), ())), precision=HI, preferred_element_type=jnp.float32
    )


def local_sums(parts):
    n_part, members, dates, width = parts.shape
    blocks = width // BLK
    summer = (
        jnp.arange(width, dtype=jnp.int32)[:, None] // BLK
        == jnp.arange(blocks, dtype=jnp.int32)[None, :]
    ).astype(jnp.bfloat16)
    flat = jnp.dot(parts.reshape(-1, width), summer, preferred_element_type=jnp.float32)
    flat = flat.reshape(n_part, members * dates, blocks)
    return jnp.moveaxis(flat, 0, 1).reshape(members * dates, n_part * blocks)


def local_predicted(sums, dates, first_block, scene_couples, targeted_tile_number):
    blocks = sums.shape[1]
    block_range = first_block + jnp.arange(blocks, dtype=jnp.int32)
    block_table = (block_range[:, None] == targeted_tile_number[None, :]).astype(jnp.float32)
    picked = mm(sums, block_table)
    timeline = jnp.arange(dates, dtype=jnp.int32)
    pair_table = (timeline[:, None] == scene_couples[1][None, :]).astype(jnp.float32) - (
        timeline[:, None] == scene_couples[0][None, :]
    ).astype(jnp.float32)
    picked = picked.reshape(-1, dates, picked.shape[1])
    return jnp.sum(picked * pair_table[None], axis=1) / BLK


def solve(gram, cross):
    n = gram.shape[0]
    factor = jnp.linalg.cholesky(jnp.eye(n, dtype=jnp.float32) + gram)
    mixing = jax.scipy.linalg.cho_solve((factor, True), cross) / math.sqrt(n - 1)
    return mixing.astype(jnp.bfloat16).astype(jnp.float32)


def combined_mixing(gram, cross_first, cross_second):
    n = gram.shape[0]
    first = solve(gram, cross_first)
    moved = first + jnp.eye(n, dtype=jnp.float32)
    moved = moved - jnp.mean(moved, axis=1, keepdims=True)
    gram_moved = mm(gram, moved)
    gram_next = tn(moved, gram_moved)
    cross_next = tn(moved, cross_second - math.sqrt(n - 1) * mm(gram, first))
    second = solve(gram_next, cross_next)
    whole = first + mm(moved, second)
    return whole - jnp.mean(whole, axis=0, keepdims=True)


def body(
    prior_motion,
    measured_motion,
    measurement_noise_stddev,
    gaussian_jitter,
    scene_couples,
    targeted_tile_number,
):
    members, dates, cells = prior_motion.shape
    n_mem = lax.axis_size("mem")
    width = cells // n_mem
    n = members * n_mem
    parts = jnp.moveaxis(prior_motion.reshape(members, dates, n_mem, width), 2, 0)
    state = lax.all_to_all(parts, "mem", split_axis=0, concat_axis=0, tiled=True)
    first_block = lax.axis_index("pix") * (cells // BLK)
    predicted = local_predicted(
        local_sums(parts), dates, first_block, scene_couples, targeted_tile_number
    )
    predicted = lax.all_gather(predicted, "mem", axis=0, tiled=True)
    in_tile = targeted_tile_number // (cells // BLK) == lax.axis_index("pix")
    spread = jnp.sqrt(jnp.float32(float(PASS_COUNT))) * measurement_noise_stddev
    scaled = (predicted - jnp.mean(predicted, axis=0, keepdims=True)) / (spread * math.sqrt(n - 1))[
        None, :
    ]
    fixed = (measured_motion[None, :] - predicted) / spread[None, :]
    misfits = [
        jnp.where(in_tile[None, :], fixed + gaussian_jitter[i].T, 0.0) for i in range(PASS_COUNT)
    ]
    right = jnp.concatenate([scaled] + misfits, axis=0)
    products = lax.dot_general(
        scaled, right, (((1,), (1,)), ((), ())), precision=HI, preferred_element_type=jnp.float32
    )
    products = lax.psum(products, "pix")
    mixing = combined_mixing(products[:, :n], products[:, n : 2 * n], products[:, 2 * n :])
    mixing = mixing.astype(jnp.bfloat16)
    rows = n * dates
    spread_mixing = (
        mixing.T[:, None, :, None] * jnp.eye(dates, dtype=jnp.bfloat16)[None, :, None, :]
    ).reshape(rows, rows)
    flat = state.reshape(rows, width)
    change = jnp.dot(spread_mixing, flat, preferred_element_type=jnp.float32)
    fresh = (flat.astype(jnp.float32) + change).astype(jnp.bfloat16)
    fresh = fresh.reshape(n_mem, members, dates, width)
    back = lax.all_to_all(fresh, "mem", split_axis=0, concat_axis=0, tiled=True)
    return jnp.moveaxis(back, 0, 2).reshape(members, dates, cells)


def solution(mesh):
    return jax.shard_map(
        body,
        mesh=mesh,
        in_specs=(P("mem", None, "pix"), P(), P(), P(), P(), P()),
        out_specs=P("mem", None, "pix"),
        check_vma=False,
    )
```

profile of v0, /device:TPU:0, one launch (start us, length us, event | category | flops | bytes accessed | tf_op | source)
XLA Modules:
  0.0 242.5 jit_solution(9956106009973401795)
XLA Ops:
  0.0 4.8 %copy.47 = bf16[4,2,16,8,2048]{4,3,1,0,2:T(8,128)(2,1)} copy(bf16[4,2,16,8,2048]{4,3,2,1,0:T(8,128)(2,1)} %bitcast.84) | data formatting | bytes 8388608 | tf_op jit(solution)/shard_map/reshape | solution.py:79
  4.8 0.0 copy-start.4
  4.8 0.0 copy-start.3
  4.8 7.3 %all-to-all-start = ((bf16[16,4,16,2048]{3,2,1,0:T(8,128)(2,1)}), bf16[16,4,16,2048]{3,2,1,0:T(8,128)(2,1)}, u32[]{:S(2)}, u32[]{:S(2)}) async-start(bf16[16,4,16,2048]{3,2,1,0:T(8,128)(2,1)} %bitcast.81), calls=%async_computation | async-start | bytes 8388608 | tf_op jit(solution)/shard_map/all_to_all | solution.py:80
  12.2 0.0 copy-done.4
  12.2 0.0 copy-done.3
  12.2 0.0 copy-done.1
  12.3 0.0 copy-start
  12.3 0.0 copy-start.2
  12.3 3.6 %convolution_bitcast_fusion = f32[1024,32]{0,1:T(8,128)S(1)} fusion(bf16[1024,2048]{1,0:T(8,128)(2,1)} %bitcast.82, s32[2048]{0:T(1024)S(1)} %add_select_fusion.1), kind=kOutput, calls=%fused_computation.10 | convolution fusion | flops 134348800 | bytes 4333568 | tf_op jit(solution)/shard_map/dot_general | solution.py:29
  15.9 0.1 reshape.162
  16.0 0.3 copy.26
  16.3 0.2 dot_general.33
  16.6 1.3 fusion.8
  17.9 72.2 %all-gather = f32[16,4,1200]{2,1,0:T(4,128)S(1)} all-gather(f32[1,4,1200]{2,1,0:T(4,128)S(1)} %multiply_bitcast_fusion), channel_id=1, replica_groups=mesh['mem'=16,'pix'=8] {'mem'}, dimensions={0}, use_global_device_ids=true | all-gather | bytes 326400 | tf_op jit(solution)/shard_map/all_gather | solution.py:85
  90.1 0.1 reshape.166
  90.3 0.1 reduce_sum.37
  90.3 0.0 copy-done
  90.3 0.0 copy-done.2
  90.4 0.1 fusion.24
  90.5 0.9 fusion.15
  91.4 25.5 %psum.7 = f32[64,192]{0,1:T(8,128)S(1)} all-reduce(f32[64,192]{0,1:T(8,128)S(1)} %fusion.15), channel_id=1, replica_groups=mesh['mem'=16,'pix'=8] {'pix'}, use_global_device_ids=true, to_apply=%region_2.3 | all-reduce | flops 12288 | bytes 98304 | tf_op jit(solution)/shard_map/psum | solution.py:99
  116.9 0.1 copy.28
  117.0 5.8 %cholesky.44 = f32[64,64]{1,0:T(8,128)S(1)} custom-call(f32[64,64]{1,0:T(8,128)S(1)} %fusion.43), custom_call_target="Cholesky" | custom-call | tf_op jit(solution)/shard_map/jit(cholesky)/cholesky | solution.py:49
  122.9 0.7 compare_reduce_fusion.1
  123.7 0.7 fusion.33
  124.4 4.9 %custom-call.8 = f32[1,64,64]{1,2,0:T(8,128)S(1)} custom-call(f32[1,64,64]{2,1,0:T(8,128)S(1)} %fusion.33), custom_call_target="InvertDiagBlocksLowerTriangular" | custom-call | tf_op jit(solution)/shard_map/jit(_cho_solve)/triangular_solve | solution.py:50
  129.3 0.2 fusion.35
  129.5 0.3 fusion.26
  129.8 0.2 fusion.31
  130.0 0.2 convolution_add_fusion.1
  130.3 0.1 copy.31
  130.4 5.8 %cholesky.55 = f32[64,64]{1,0:T(8,128)S(1)} custom-call(f32[64,64]{1,0:T(8,128)S(1)} %fusion.40), custom_call_target="Cholesky" | custom-call | tf_op jit(solution)/shard_map/jit(cholesky)/cholesky | solution.py:49
  136.2 0.7 compare_reduce_fusion
  137.0 0.7 fusion.34
  137.7 4.9 %custom-call.9 = f32[1,64,64]{1,2,0:T(8,128)S(1)} custom-call(f32[1,64,64]{2,1,0:T(8,128)S(1)} %fusion.34), custom_call_target="InvertDiagBlocksLowerTriangular" | custom-call | tf_op jit(solution)/shard_map/jit(_cho_solve)/triangular_solve | solution.py:50
  142.6 0.1 fusion.11
  142.7 0.2 fusion.28
  142.9 0.2 fusion.38
  143.2 0.2 fusion.13
  143.4 0.3 fusion.60
  143.7 0.1 fusion.46
  143.8 5.9 %broadcast_multiply_fusion = bf16[64,16,64,16]{3,2,1,0:T(8,128)(2,1)} fusion(bf16[16,16]{1,0:T(8,128)(2,1)S(1)} %fusion.56, bf16[64,64]{1,0:T(8,128)(2,1)S(1)} %fusion.46), kind=kLoop, calls=%fused_computation.1 | loop fusion | flops 1048576 | bytes 2105856 | tf_op jit(solution)/shard_map/mul | solution.py:104
  149.7 29.1 %mul.60 = bf16[1024,1024]{1,0:T(8,128)(2,1)S(1)} reshape(bf16[64,16,64,16]{3,2,1,0:T(8,128)(2,1)} %broadcast_multiply_fusion) | data formatting | bytes 4194304 | tf_op jit(solution)/shard_map/mul | solution.py:104
  178.8 0.0 all-to-all-done
  178.8 8.0 %add_convert_fusion = bf16[1024,2048]{1,0:T(8,128)(2,1)S(1)} fusion(bf16[1024,2048]{1,0:T(8,128)(2,1)} %bitcast.1, bf16[1024,1024]{1,0:T(8,128)(2,1)S(1)} %mul.60), kind=kOutput, calls=%fused_computation | convolution fusion | flops 4301258752 | bytes 10485760 | tf_op jit(solution)/shard_map/dot_general | solution.py:107
  186.9 53.3 %all_to_all.10 = bf16[16,4,16,2048]{3,2,1,0:T(8,128)(2,1)S(1)} all-to-all(bf16[16,4,16,2048]{3,2,1,0:T(8,128)(2,1)S(1)} %bitcast.85), channel_id=1, replica_groups=mesh['mem'=16,'pix'=8] {'mem'}, dimensions={0} | all-to-all | bytes 8388608 | tf_op jit(solution)/shard_map/all_to_all | solution.py:110
  240.2 2.3 copy.43
  (17 shorter events, 0.2 us)
Async XLA Ops:
  4.8 7.4 %copy-start.4 = (s32[1200]{0:T(1024)S(1)}, s32[1200]{0:T(1024)}, u32[]{:S(2)}) copy-start(s32[1200]{0:T(1024)} %param.14) | copy-start | bytes 14404
  4.8 7.4 %copy-start.3 = (f32[1200]{0:T(1024)S(1)}, f32[1200]{0:T(1024)}, u32[]{:S(2)}) copy-start(f32[1200]{0:T(1024)} %param.11) | copy-start | bytes 14404
  4.8 7.4 %copy-start.1 = (s32[2,1200]{1,0:T(2,128)S(1)}, s32[2,1200]{1,0:T(2,128)}, u32[]{:S(2)}) copy-start(s32[2,1200]{1,0:T(2,128)} %param.13) | copy-start | bytes 28804
  4.8 174.0 %all-to-all-start = ((bf16[16,4,16,2048]{3,2,1,0:T(8,128)(2,1)}), bf16[16,4,16,2048]{3,2,1,0:T(8,128)(2,1)}, u32[]{:S(2)}, u32[]{:S(2)}) async-start(bf16[16,4,16,2048]{3,2,1,0:T(8,128)(2,1)} %bitcast.81), calls=%async_computation | async-start | bytes 8388608 | tf_op jit(solution)/shard_map/all_to_all | solution.py:80
  12.3 78.1 %copy-start = (f32[2,1200,64]{1,2,0:T(8,128)S(1)}, f32[2,1200,64]{1,2,0:T(8,128)}, u32[]{:S(2)}) copy-start(f32[2,1200,64]{1,2,0:T(8,128)} %param.12) | copy-start | bytes 1843204
  12.3 78.1 %copy-start.2 = (f32[1200]{0:T(1024)S(1)}, f32[1200]{0:T(1024)}, u32[]{:S(2)}) copy-start(f32[1200]{0:T(1024)} %param.10) | copy-start | bytes 14404
where the time goes:
time: 243 us
  blocking collectives  151 us (62%)
  local copies, waits for them, and re-layouts  37.1 us (15%)
  other arithmetic  30.7 us (13%)
  matrix products  15.9 us (7%)
  starting transfers between devices  7.33 us (3%)
    all_gather x1, blocking collectives, body(): predicted = lax.all_gather(predicted, 'mem', axis=0, tiled=True)  72.2 us
    all_to_all x1, blocking collectives, body(): back = lax.all_to_all(fresh, 'mem', split_axis=0, concat_axis=0, tiled=True)  53.3 us
    mul x1, local copies, waits for them, and re-layouts, body(): mixing.T[:, None, :, None]  29.1 us
    psum x1, blocking collectives, body(): products = lax.psum(products, 'pix')  25.5 us
    another operation x6, other arithmetic, solve(): factor = jnp.linalg.cholesky(jnp.eye(n, dtype=jnp.float32) + gram)  13.2 us
    another operation x4, other arithmetic, solve(): jax.scipy.linalg.cho_solve((factor, True), cross) / math.sqrt(n - 1)  11.2 us
    dot_general x1, matrix products, body(): change = jnp.dot(spread_mixing, flat, preferred_element_type=jnp.float32)  8.04 us
    all_to_all x1, starting transfers between devices, body(): lax.all_to_all(parts, 'mem', split_axis=0, concat_axis=0, tiled=True)  7.33 us
  transfers between devices with their start and end apart: 1, of which 0 were waited for; matrix products, arithmetic and copies ran while one was open for 28% of the time, Pallas kernels for 0%

commit v1 on v0

--- a/solution.py
+++ b/solution.py
@@ -96,7 +96,7 @@
     products = lax.dot_general(
         scaled, right, (((1,), (1,)), ((), ())), precision=HI, preferred_element_type=jnp.float32
     )
-    products = lax.psum(products, "pix")
+    products = jnp.sum(lax.all_gather(products, "pix"), axis=0)
     mixing = combined_mixing(products[:, :n], products[:, n : 2 * n], products[:, 2 * n :])
     mixing = mixing.astype(jnp.bfloat16)
     rows = n * dates

time: 243 us -> 235 us (0.967)
  blocking collectives: 151 us -> 143 us
    psum x1 -> x0, blocking collectives: 25.5 us -> none  [body(): products = lax.psum(products, 'pix')]
    all_gather x0 -> x1, blocking collectives: none -> 14.5 us  [body(): products = jnp.sum(lax.all_gather(products, 'pix'), axis=0)]
    all_to_all x1, blocking collectives: 53.3 us -> 56.4 us  [body(): back = lax.all_to_all(fresh, 'mem', split_axis=0, concat_axis=0, tiled=True)]
  transfers between devices with their start and end apart: 1 -> 1, of which waited for: 0 -> 0; matrix products, arithmetic and copies ran while one was open for 28% -> 29% of each run, Pallas kernels for 0% -> 0%
where the time goes in v1:
time: 235 us
  blocking collectives  143 us (61%)
  local copies, waits for them, and re-layouts  37.2 us (16%)
  other arithmetic  30.7 us (13%)
  matrix products  16 us (7%)
  starting transfers between devices  7.33 us (3%)
    all_gather x1, blocking collectives, body(): predicted = lax.all_gather(predicted, 'mem', axis=0, tiled=True)  72.2 us
    all_to_all x1, blocking collectives, body(): back = lax.all_to_all(fresh, 'mem', split_axis=0, concat_axis=0, tiled=True)  56.4 us
    mul x1, local copies, waits for them, and re-layouts, body(): mixing.T[:, None, :, None]  29.1 us
    all_gather x1, blocking collectives, body(): products = jnp.sum(lax.all_gather(products, 'pix'), axis=0)  14.5 us
    another operation x6, other arithmetic, solve(): factor = jnp.linalg.cholesky(jnp.eye(n, dtype=jnp.float32) + gram)  13.2 us
    another operation x4, other arithmetic, solve(): jax.scipy.linalg.cho_solve((factor, True), cross) / math.sqrt(n - 1)  11.2 us
    dot_general x1, matrix products, body(): change = jnp.dot(spread_mixing, flat, preferred_element_type=jnp.float32)  8.04 us
    all_to_all x1, starting transfers between devices, body(): lax.all_to_all(parts, 'mem', split_axis=0, concat_axis=0, tiled=True)  7.33 us
  transfers between devices with their start and end apart: 1, of which 0 were waited for; matrix products, arithmetic and copies ran while one was open for 29% of the time, Pallas kernels for 0%

profile of v1, /device:TPU:0, one launch (start us, length us, event | category | flops | bytes accessed | tf_op | source)
XLA Modules:
  0.0 234.7 jit_solution(2026340492678154489)
XLA Ops:
  0.0 4.8 %copy.43 = bf16[4,2,16,8,2048]{4,3,1,0,2:T(8,128)(2,1)} copy(bf16[4,2,16,8,2048]{4,3,2,1,0:T(8,128)(2,1)} %bitcast.85) | data formatting | bytes 8388608 | tf_op jit(solution)/shard_map/reshape | solution.py:79
  4.8 0.0 copy-start.4
  4.8 7.3 %all-to-all-start = ((bf16[16,4,16,2048]{3,2,1,0:T(8,128)(2,1)}), bf16[16,4,16,2048]{3,2,1,0:T(8,128)(2,1)}, u32[]{:S(2)}, u32[]{:S(2)}) async-start(bf16[16,4,16,2048]{3,2,1,0:T(8,128)(2,1)} %bitcast.82), calls=%async_computation | async-start | bytes 8388608 | tf_op jit(solution)/shard_map/all_to_all | solution.py:80
  12.2 0.0 copy-done.4
  12.2 0.0 copy-done.3
  12.2 0.0 copy-done.1
  12.3 0.0 copy-start
  12.3 0.0 copy-start.2
  12.3 3.6 %convolution_bitcast_fusion = f32[1024,32]{0,1:T(8,128)S(1)} fusion(bf16[1024,2048]{1,0:T(8,128)(2,1)} %bitcast.83, s32[2048]{0:T(1024)S(1)} %add_select_fusion.1), kind=kOutput, calls=%fused_computation.10 | convolution fusion | flops 134348800 | bytes 4333568 | tf_op jit(solution)/shard_map/dot_general | solution.py:29
  15.9 0.1 reshape.162
  16.0 0.3 copy.24
  16.3 0.2 dot_general.33
  16.6 1.3 fusion.8
  17.9 72.2 %all-gather.1 = f32[16,4,1200]{2,1,0:T(4,128)S(1)} all-gather(f32[1,4,1200]{2,1,0:T(4,128)S(1)} %multiply_bitcast_fusion), channel_id=1, replica_groups=mesh['mem'=16,'pix'=8] {'mem'}, dimensions={0}, use_global_device_ids=true | all-gather | bytes 326400 | tf_op jit(solution)/shard_map/all_gather | solution.py:85
  90.1 0.1 reshape.167
  90.3 0.1 reduce_sum.46
  90.3 0.0 copy-done
  90.3 0.0 copy-done.2
  90.4 0.1 fusion.24
  90.5 1.1 fusion.15
  91.5 14.5 %all-gather = f32[512,192]{1,0:T(8,128)S(1)} all-gather(f32[64,192]{1,0:T(8,128)S(1)} %fusion.15), channel_id=2, replica_groups=mesh['mem'=16,'pix'=8] {'pix'}, dimensions={0}, use_global_device_ids=true | all-gather | bytes 442368 | tf_op jit(solution)/shard_map/all_gather | solution.py:99
  106.1 0.1 copy.37
  106.2 0.1 copy.26
  106.3 5.8 %cholesky.44 = f32[64,64]{1,0:T(8,128)S(1)} custom-call(f32[64,64]{1,0:T(8,128)S(1)} %fusion.43), custom_call_target="Cholesky" | custom-call | tf_op jit(solution)/shard_map/jit(cholesky)/cholesky | solution.py:49
  112.2 0.7 compare_reduce_fusion.1
  112.9 0.7 fusion.33
  113.6 4.9 %custom-call.8 = f32[1,64,64]{1,2,0:T(8,128)S(1)} custom-call(f32[1,64,64]{2,1,0:T(8,128)S(1)} %fusion.33), custom_call_target="InvertDiagBlocksLowerTriangular" | custom-call | tf_op jit(solution)/shard_map/jit(_cho_solve)/triangular_solve | solution.py:50
  118.5 0.3 fusion.35
  118.8 0.3 fusion.26
  119.0 0.2 fusion.31
  119.2 0.2 convolution_add_fusion.1
  119.5 0.1 copy.29
  119.6 5.8 %cholesky.55 = f32[64,64]{1,0:T(8,128)S(1)} custom-call(f32[64,64]{1,0:T(8,128)S(1)} %fusion.40), custom_call_target="Cholesky" | custom-call | tf_op jit(solution)/shard_map/jit(cholesky)/cholesky | solution.py:49
  125.5 0.7 compare_reduce_fusion
  126.2 0.7 fusion.34
  126.9 4.9 %custom-call.9 = f32[1,64,64]{1,2,0:T(8,128)S(1)} custom-call(f32[1,64,64]{2,1,0:T(8,128)S(1)} %fusion.34), custom_call_target="InvertDiagBlocksLowerTriangular" | custom-call | tf_op jit(solution)/shard_map/jit(_cho_solve)/triangular_solve | solution.py:50
  131.8 0.2 fusion.11
  132.0 0.2 fusion.28
  132.1 0.2 fusion.38
  132.4 0.2 fusion.13
  132.6 0.3 fusion.60
  132.9 0.1 fusion.44
  133.0 5.9 %broadcast_multiply_fusion = bf16[64,16,64,16]{3,2,1,0:T(8,128)(2,1)} fusion(bf16[16,16]{1,0:T(8,128)(2,1)S(1)} %fusion.54, bf16[64,64]{1,0:T(8,128)(2,1)S(1)} %fusion.44), kind=kLoop, calls=%fused_computation.1 | loop fusion | flops 1048576 | bytes 2105856 | tf_op jit(solution)/shard_map/mul | solution.py:104
  138.9 29.1 %mul.60 = bf16[1024,1024]{1,0:T(8,128)(2,1)S(1)} reshape(bf16[64,16,64,16]{3,2,1,0:T(8,128)(2,1)} %broadcast_multiply_fusion) | data formatting | bytes 4194304 | tf_op jit(solution)/shard_map/mul | solution.py:104
  168.0 0.0 all-to-all-done
  168.0 8.0 %add_convert_fusion = bf16[1024,2048]{1,0:T(8,128)(2,1)S(1)} fusion(bf16[1024,2048]{1,0:T(8,128)(2,1)} %bitcast.1, bf16[1024,1024]{1,0:T(8,128)(2,1)S(1)} %mul.60), kind=kOutput, calls=%fused_computation | convolution fusion | flops 4301258752 | bytes 10485760 | tf_op jit(solution)/shard_map/dot_general | solution.py:107
  176.1 56.4 %all_to_all.10 = bf16[16,4,16,2048]{3,2,1,0:T(8,128)(2,1)S(1)} all-to-all(bf16[16,4,16,2048]{3,2,1,0:T(8,128)(2,1)S(1)} %bitcast.86), channel_id=1, replica_groups=mesh['mem'=16,'pix'=8] {'mem'}, dimensions={0} | all-to-all | bytes 8388608 | tf_op jit(solution)/shard_map/all_to_all | solution.py:110
  232.4 2.3 copy.39
  (20 shorter events, 0.3 us)
Async XLA Ops:
  4.8 7.4 %copy-start.4 = (s32[1200]{0:T(1024)S(1)}, s32[1200]{0:T(1024)}, u32[]{:S(2)}) copy-start(s32[1200]{0:T(1024)} %param.14) | copy-start | bytes 14404
  4.8 7.4 %copy-start.3 = (f32[1200]{0:T(1024)S(1)}, f32[1200]{0:T(1024)}, u32[]{:S(2)}) copy-start(f32[1200]{0:T(1024)} %param.11) | copy-start | bytes 14404
  4.8 7.4 %copy-start.1 = (s32[2,1200]{1,0:T(2,128)S(1)}, s32[2,1200]{1,0:T(2,128)}, u32[]{:S(2)}) copy-start(s32[2,1200]{1,0:T(2,128)} %param.13) | copy-start | bytes 28804
  4.8 163.2 %all-to-all-start = ((bf16[16,4,16,2048]{3,2,1,0:T(8,128)(2,1)}), bf16[16,4,16,2048]{3,2,1,0:T(8,128)(2,1)}, u32[]{:S(2)}, u32[]{:S(2)}) async-start(bf16[16,4,16,2048]{3,2,1,0:T(8,128)(2,1)} %bitcast.82), calls=%async_computation | async-start | bytes 8388608 | tf_op jit(solution)/shard_map/all_to_all | solution.py:80
  12.3 78.1 %copy-start = (f32[2,1200,64]{1,2,0:T(8,128)S(1)}, f32[2,1200,64]{1,2,0:T(8,128)}, u32[]{:S(2)}) copy-start(f32[2,1200,64]{1,2,0:T(8,128)} %param.12) | copy-start | bytes 1843204
  12.3 78.1 %copy-start.2 = (f32[1200]{0:T(1024)S(1)}, f32[1200]{0:T(1024)}, u32[]{:S(2)}) copy-start(f32[1200]{0:T(1024)} %param.10) | copy-start | bytes 14404
